TPU v7x, 32 devices: a whole 2x2x4 slice. The times are simulated.
32 devices in a mesh: data: 32 (over z, y, x, core).
Axes of the slice: x: 2, y: 2, z: 4, core: 2. Of those that a mesh axis runs over, the one named last changes fastest.
Arguments:
- tok_ids: int32 [32768], P('data')
- grad_out: bfloat16 [32768, 1024], P('data')
- n_real: int32 [32], P('data')
- embed_table: bfloat16 [50265, 1024], replicated
- w_in: bfloat16 [1024, 4096], replicated
- w_out: bfloat16 [4096, 1024], replicated
Outputs:
- output 1: float32 [50265, 1024], replicated
- output 2: float32 [1024, 4096], replicated
- output 3: float32 [4096, 1024], replicated
All inputs are finite; a program needn't handle non-finite values.
Results may differ from a plain program's by a relative error of at most 0.00849531.
Values are sent between devices in bfloat16 or wider.
A program may use at most 1.5 GiB of HBM per device.

v0:
```python
import math
import jax
import jax.numpy as jnp
from jax import lax
from jax.sharding import PartitionSpec as P

GELU_A = 0.044715
GELU_C = math.sqrt(2.0 / math.pi)


def local_grads(x_rows, grad_out, keep_mask, w_in, w_out):
    dy_kept = jnp.where(keep_mask, grad_out, jnp.zeros_like(grad_out))
    pre_act = jnp.dot(x_rows, w_in, preferred_element_type=jnp.float32).astype(jnp.bfloat16)
    z_val = pre_act.astype(jnp.float32)
    tanh_val = jnp.tanh(GELU_C * (z_val + GELU_A * z_val * z_val * z_val))
    act_bf16 = (0.5 * z_val * (1.0 + tanh_val)).astype(jnp.bfloat16)
    slope_val = 0.5 * (1.0 + tanh_val) + 0.5 * z_val * (1.0 - tanh_val * tanh_val) * GELU_C * (1.0 + 3.0 * GELU_A * z_val * z_val)
    grad_w_out = jnp.einsum('tf,td->fd', act_bf16, dy_kept, preferred_element_type=jnp.float32)
    grad_act = jnp.einsum('td,fd->tf', dy_kept, w_out, preferred_element_type=jnp.float32).astype(jnp.bfloat16)
    grad_pre = (grad_act.astype(jnp.float32) * slope_val).astype(jnp.bfloat16)
    grad_w_in = jnp.einsum('td,tf->df', x_rows, grad_pre, preferred_element_type=jnp.float32)
    grad_x = (dy_kept.astype(jnp.float32) + jnp.einsum('tf,df->td', grad_pre, w_in, preferred_element_type=jnp.float32)).astype(jnp.bfloat16)
    return grad_x, grad_w_in, grad_w_out


def solution(mesh):
    def per_device(tok_ids, grad_out, n_real, embed_table, w_in, w_out):
        keep_mask = (jnp.arange(tok_ids.shape[0]) < n_real[0])[:, None]
        x_rows = jnp.take(embed_table, tok_ids, axis=0)
        grad_x, part_in, part_out = local_grads(x_rows, grad_out, keep_mask, w_in, w_out)
        grad_w_in = lax.psum(part_in, 'data')
        grad_w_out = lax.psum(part_out, 'data')
        all_ids = lax.all_gather(tok_ids, 'data', tiled=True)
        all_rows = lax.all_gather(grad_x, 'data', tiled=True)
        grad_table = jax.ops.segment_sum(all_rows.astype(jnp.float32), all_ids, num_segments=embed_table.shape[0])
        return grad_table, grad_w_in, grad_w_out

    return jax.shard_map(per_device, mesh=mesh, in_specs=(P('data'), P('data', None), P('data'), P(), P(), P()), out_specs=(P(), P(), P()), check_vma=False)
```

profile of v0, /device:TPU:0, one launch (start us, length us, event | category | flops | bytes accessed | tf_op | source)
XLA Modules:
  0.0 1177.2 jit_solution(15939012064049790060)
XLA Ops:
  7.2 0.0 all-gather.2.cloned.1.call-start
  7.2 0.7 fusion.24
  7.9 0.7 compare_and_fusion
  9.3 14.8 %gather_fusion = bf16[1024,1024]{1,0:T(8,128)(2,1)S(1)} fusion(bf16[50265,1024]{1,0:T(8,128)(2,1)} %param.9, s32[1024]{0:T(1024)S(1)} %fusion.24), kind=kCustom, calls=%fused_computation | custom fusion | bytes 4198400 | tf_op jit(solution)/shard_map/jit(_take)/gather | solution.py:29
  24.0 0.0 copy-start.2
  24.1 14.8 %convolution_convert_fusion = bf16[1024,4096]{1,0:T(8,128)(2,1)} fusion(bf16[1024,4096]{1,0:T(8,128)(2,1)} %param.10, bf16[1024,1024]{1,0:T(8,128)(2,1)S(1)} %gather_fusion, pred[1024]{0:T(1024)(128)(4,1)S(1)} %compare_and_fusion), kind=kOutput, calls=%fused_computation.29 | convolution fusion | flops 8595177472 | bytes 18875392 | tf_op jit(solution)/shard_map/dot_general | solution.py:13
  38.8 0.0 copy-done.2
  38.8 21.4 %fusion.12 = bf16[1024,4096]{1,0:T(8,128)(2,1)} fusion(bf16[1024,4096]{1,0:T(8,128)(2,1)} %convolution_convert_fusion, bf16[4096,1024]{1,0:T(8,128)(2,1)S(1)} %copy-done.2, bf16[1024,1024]{1,0:T(8,128)(2,1)} %param.7, pred[1024]{0:T(1024)(128)(4,1)S(1)} %iota_compare_fusion), kind=kOutput, calls=%fused_computation.19 | convolution fusion | flops 8683257856 | bytes 27264000 | tf_op jit(solution)/shard_map/td,fd->tf/dot_general | solution.py:19
  60.3 15.3 %add_convert_fusion = bf16[1024,1024]{1,0:T(8,128)(2,1)} fusion(bf16[1024,4096]{1,0:T(8,128)(2,1)} %fusion.12, bf16[1024,4096]{1,0:T(8,128)(2,1)} %param.10, bf16[1024,1024]{1,0:T(8,128)(2,1)} %param.7, pred[1024]{0:T(1024)(128)(4,1)S(1)} %iota_compare_fusion), kind=kOutput, calls=%fused_computation.30 | convolution fusion | flops 8594128896 | bytes 20972544 | tf_op jit(solution)/shard_map/tf,df->td/dot_general | solution.py:22
  75.6 0.0 all-gather.2.cloned.1.call-update
  75.7 0.0 all-reduce.3.cloned.1.call-start
  75.7 0.0 copy-start.3
  75.7 15.7 %fusion.23 = f32[1024,4096]{1,0:T(8,128)} fusion(bf16[1024,4096]{1,0:T(8,128)(2,1)} %fusion.12, bf16[1024,1024]{1,0:T(8,128)(2,1)S(1)} %gather_fusion, pred[1024]{0:T(1024)(128)(4,1)S(1)} %compare_and_fusion), kind=kOutput, calls=%fused_computation.33 | convolution fusion | flops 8590983168 | bytes 27264000 | tf_op jit(solution)/shard_map/td,tf->df/dot_general | solution.py:21
  91.4 0.0 copy-done.3
  91.4 18.6 %fusion.17 = f32[4096,1024]{1,0:T(8,128)} fusion(bf16[1024,4096]{1,0:T(8,128)(2,1)} %convolution_convert_fusion, bf16[1024,1024]{1,0:T(8,128)(2,1)S(1)} %copy-done.3, pred[1024]{0:T(1024)(128)(4,1)S(1)} %iota_compare_fusion), kind=kOutput, calls=%fused_computation.24 | convolution fusion | flops 8632926208 | bytes 27264000 | tf_op jit(solution)/shard_map/tf,td->fd/dot_general | solution.py:18
  110.0 0.0 copy-start.1
  110.0 0.0 all-reduce.3.cloned.1.call-update
  110.1 0.7 copy-done.1
  110.7 55.3 %all_gather.6 = s32[32768]{0:T(1024)S(1)} all-gather(s32[1024]{0:T(1024)S(1)} %copy-done.1), channel_id=1, replica_groups=mesh['data'=32] {'data'}, dimensions={0}, use_global_device_ids=true | all-gather | bytes 135168 | tf_op jit(solution)/shard_map/all_gather | solution.py:33
  166.0 10.4 sort
  176.5 258.5 %all-gather.2.cloned.1.call-done = bf16[32768,1024]{1,0:T(8,128)(2,1)} async-done(((bf16[1024,1024]{1,0:T(8,128)(2,1)}), bf16[32768,1024]{1,0:T(8,128)(2,1)}) %all-gather.2.cloned.1.call-update) | async-done | bytes 67108880 | tf_op jit(solution)/shard_map/all_gather | solution.py:34
  435.0 67.5 %convert_element_type.34 = f32[32768,1024]{1,0:T(8,128)} convert(bf16[32768,1024]{1,0:T(8,128)(2,1)} %all-gather.2.cloned.1.call-done) | non-fusion elementwise | flops 33554432 | bytes 201326592 | tf_op jit(solution)/shard_map/convert_element_type | solution.py:35
  502.5 644.9 %scatter_custom_fusion = f32[50265,1024]{1,0:T(8,128)} fusion(s32[32768]{0:T(1024)S(1)} %get-tuple-element.3, f32[32768,1024]{1,0:T(8,128)} %convert_element_type.34, s32[32768]{0:T(1024)S(1)} %broadcast_clamp_fusion, f32[]{:T(128)} %constant.11.clone.1), kind=kCustom, calls=%fused_computation.3 | custom fusion | flops 33554432 | bytes 205885952 | tf_op jit(solution)/shard_map/scatter-add | solution.py:35
  1147.4 0.0 all-reduce.3.cloned.1.call-done
  1147.4 0.0 copy-start
  1147.4 12.6 %copy.12 = f32[1024,4096]{1,0:T(8,128)} copy(f32[1024,4096]{1,0:T(8,128)} %get-tuple-element.8) | data formatting | bytes 33554432
  1160.0 3.8 copy-done
  1163.8 6.2 copy.13
  (3 shorter events, 0.0 us)
Async XLA Ops:
  7.2 427.8 %all-gather.2.cloned.1.call-start = ((), (), s32[]{:S(2)}) async-start(), calls=%async_computation | async-start | bytes 69206016 | tf_op jit(solution)/shard_map/all_gather | solution.py:34
  24.0 14.8 %copy-start.2 = (bf16[4096,1024]{1,0:T(8,128)(2,1)S(1)}, bf16[4096,1024]{1,0:T(8,128)(2,1)}, u32[]{:S(2)}) copy-start(bf16[4096,1024]{1,0:T(8,128)(2,1)} %param.11) | copy-start | bytes 25165828
  75.7 1071.7 %all-reduce.3.cloned.1.call-start = ((), (), s32[]{:S(2)}) async-start(), calls=%async_computation.1 | async-start | bytes 67108864 | tf_op jit(solution)/shard_map/psum | solution.py:31
  75.7 15.7 %copy-start.3 = (bf16[1024,1024]{1,0:T(8,128)(2,1)S(1)}, bf16[1024,1024]{1,0:T(8,128)(2,1)}, u32[]{:S(2)}) copy-start(bf16[1024,1024]{1,0:T(8,128)(2,1)} %param.7) | copy-start | bytes 6291460
  110.0 0.7 copy-start.1
  1147.4 16.4 %copy-start = (f32[4096,1024]{1,0:T(8,128)S(1)}, f32[4096,1024]{1,0:T(8,128)}, u32[]{:S(2)}) copy-start(f32[4096,1024]{1,0:T(8,128)} %get-tuple-element.9) | copy-start | bytes 50331652
Sparse Core Ops, SparseCore 0:
  75.8 359.1 all-gather.1
  442.0 494.7 all-reduce.2
where the time goes:
time: 1190 us; the launch traced here: 1180 us
  other arithmetic  724 us (61%)
  waiting for transfers between devices  259 us (22%)
  matrix products  85.9 us (7%)
  blocking collectives  55.3 us (5%)
  local copies, waits for them, and re-layouts  38 us (3%)
  between operations  15.1 us (1%)
    scatter-add x3, other arithmetic, per_device(): jax.ops.segment_sum(all_rows.astype(jnp.float32), all_ids, num_segments=e...  655 us
    all_gather x1, waiting for transfers between devices, per_device(): all_rows = lax.all_gather(grad_x, 'data', tiled=True)  259 us
    convert_element_type x1, other arithmetic, per_device(): all_rows.astype(jnp.float32)  67.5 us
    all_gather x1, blocking collectives, per_device(): all_ids = lax.all_gather(tok_ids, 'data', tiled=True)  55.3 us
  transfers between devices with their start and end apart: 2, of which 1 were waited for; matrix products, arithmetic and copies ran while one was open for 64% of the time, Pallas kernels for 0%

commit v1 on v0

v1 whole, which is shorter than its diff:
```python
import math
import jax
import jax.numpy as jnp
from jax import lax
from jax.experimental import pallas as pl
from jax.experimental.pallas import tpu as pltpu
from jax.sharding import PartitionSpec as P


GELU_A = 0.044715
GELU_C = math.sqrt(2.0 / math.pi)
F32 = jnp.float32
BF16 = jnp.bfloat16

TOK = 1024
DIM = 1024
FFN = 4096
VOCAB = 50265
UNIQ = 256
BLOCK = UNIQ + 8
NDEV = 32
TABLE_ROWS = 1024
UNROLL = 8
TABLE_STEPS = -(-VOCAB // TABLE_ROWS)


def device_index(z, y, x, c):
    return ((z * 2 + y) * 2 + x) * 2 + c


COORDS = [(z, y, x, c) for z in range(4) for y in range(2) for x in range(2) for c in range(2)]
PAIRS_X = [(device_index(z, y, x, c), device_index(z, y, 1 - x, c)) for z, y, x, c in COORDS]
PAIRS_Y = [(device_index(z, y, x, c), device_index(z, 1 - y, x, c)) for z, y, x, c in COORDS]
PAIRS_C = [(device_index(z, y, x, c), device_index(z, y, x, 1 - c)) for z, y, x, c in COORDS]


def pairs_up(senders):
    return [(device_index(z, y, x, c), device_index(z + 1, y, x, c)) for z, y, x, c in COORDS if z in senders]


def pairs_down(senders):
    return [(device_index(z, y, x, c), device_index(z - 1, y, x, c)) for z, y, x, c in COORDS if z in senders]


def send(arr, pairs):
    return lax.ppermute(arr, 'data', pairs)


def pick_at(arr, i, axis):
    return lax.dynamic_index_in_dim(arr, i, axis=axis, keepdims=False)


def scatter_sum(part, x, y, z):
    rows, width = part.shape
    k = rows // 32
    part = part.reshape(2, 2, 4, 2, k, width)
    ox, oy = 1 - x, 1 - y

    def cut(arr, i, j, half):
        sizes = (arr.shape[0] if i is None else 1, arr.shape[1] if j is None else 1, 4, 1, k, width)
        return lax.dynamic_slice(arr, (0 if i is None else i, 0 if j is None else j, 0, half, 0, 0), sizes)

    away_a = cut(part, ox, None, 0)
    away_b = cut(part, None, oy, 1)
    got_a = send(away_a, PAIRS_X)
    got_b = send(away_b, PAIRS_Y)
    away_a = cut(part, x, oy, 0) + cut(got_a, None, oy, 0)
    away_b = cut(part, ox, y, 1) + cut(got_b, ox, None, 0)
    last_a = send(away_a, PAIRS_Y)
    last_b = send(away_b, PAIRS_X)
    sum_a = cut(part, x, y, 0) + cut(got_a, None, y, 0) + last_a
    sum_b = cut(part, x, y, 1) + cut(got_b, x, None, 0) + last_b
    col = jnp.concatenate([sum_a, sum_b], axis=3).reshape(4, 2, k, width)

    def shard(i):
        return pick_at(col, jnp.clip(i, 0, 3), 0)

    up = send(shard(z + 3), pairs_up([0]))
    down = send(shard(z - 3), pairs_down([3]))
    up = send(shard(z + 2) + up, pairs_up([0, 1]))
    down = send(shard(z - 2) + down, pairs_down([3, 2]))
    up = send(shard(z + 1) + up, pairs_up([0, 1, 2]))
    down = send(shard(z - 1) + down, pairs_down([3, 2, 1]))
    return shard(z) + up + down


def gather_column(block, z):
    up, down = [block], [block]
    for step in range(1, 4):
        up.append(send(up[-1], pairs_up(range(step - 1, 3))))
        down.append(send(down[-1], pairs_down(range(1, 5 - step))))
    seven = jnp.stack([up[3], up[2], up[1], block, down[1], down[2], down[3]])
    return lax.dynamic_slice_in_dim(seven, 3 - z, 4, axis=0)


def gather_plane(col):
    gx = send(col, PAIRS_X)
    gy = send(col, PAIRS_Y)
    low = send(gy[:2], PAIRS_X)
    high = send(gx[2:], PAIRS_Y)
    return [col, gx, gy, low, high]


def cross(pieces):
    return [send(p, PAIRS_C) for p in pieces]


def blank(shape):
    return pl.pallas_call(lambda ref: None, out_shape=jax.ShapeDtypeStruct(shape, F32), out_specs=pl.BlockSpec(memory_space=pl.ANY), name='blank')()


def gather_weight(shard, x, y, z, c):
    width = shard.shape[-1]
    k = shard.shape[1]
    pieces = gather_plane(gather_column(shard, z))
    out = blank((64 * k, width))
    ox, oy = 1 - x, 1 - y
    places = ((x, y, 0), (ox, y, 0), (x, oy, 0), (ox, oy, 0), (ox, oy, 2))
    for lane, parts in ((c, pieces), (1 - c, cross(pieces))):
        for p, (i, j, first) in zip(parts, places):
            out = lax.dynamic_update_slice_in_dim(out, p.reshape(-1, width), lane * 32 * k + ((i * 2 + j) * 8 + first * 2) * k, axis=0)
    return out


def table_kernel(start_ref, entry_ref, row_ref, *refs):
    pieces, (out_ref, rows, sem) = refs[:-3], refs[-3:]
    step = pl.program_id(0)

    @pl.when(step == 0)
    def _():
        base = 0
        copies = []
        for piece in pieces:
            for j in range(piece.shape[0]):
                copies.append(pltpu.make_async_copy(piece.at[j], rows.at[pl.ds(base, BLOCK)], sem.at[len(copies)]))
                base += BLOCK
        for cp in copies:
            cp.start()
        for cp in copies:
            cp.wait()

    out_ref[...] = jnp.zeros_like(out_ref)

    def add_row(i, acc):
        entry = entry_ref[i]
        r = entry & (TABLE_ROWS - 1)
        acc = rows[pl.ds(row_ref[i], 1), :] + jnp.where(entry >= TABLE_ROWS, acc, 0.0)
        out_ref[pl.ds(r, 1), :] = acc
        return acc

    def add_rows(g, acc):
        for k in range(UNROLL):
            acc = add_row(first + g * UNROLL + k, acc)
        return acc

    first, last = start_ref[step], start_ref[step + 1]
    whole = (last - first) // UNROLL
    acc = lax.fori_loop(0, whole, add_rows, jnp.zeros((1, DIM), F32))
    lax.fori_loop(first + whole * UNROLL, last, add_row, acc)


def build_table(pieces):
    keys = jnp.concatenate([p[:, UNIQ, :UNIQ].reshape(-1) for p in pieces]).astype(jnp.int32)
    n = keys.shape[0]
    place = jnp.arange(n, dtype=jnp.int32)
    place = (place // UNIQ) * BLOCK + place % UNIQ
    keys, place = lax.sort((keys, place), num_keys=1)
    ids = keys // NDEV
    same = jnp.concatenate([jnp.zeros((1,), bool), ids[1:] == ids[:-1]])
    entry = ids % TABLE_ROWS + jnp.where(same, TABLE_ROWS, 0)
    bounds = jnp.arange(TABLE_STEPS + 1, dtype=jnp.int32) * TABLE_ROWS
    starts = jnp.sum(ids[None, :] < bounds[:, None], axis=1, dtype=jnp.int32)
    return pl.pallas_call(
        table_kernel,
        out_shape=jax.ShapeDtypeStruct((VOCAB, DIM), F32),
        grid_spec=pltpu.PrefetchScalarGridSpec(
            num_scalar_prefetch=3,
            grid=(TABLE_STEPS,),
            in_specs=[pl.BlockSpec(memory_space=pl.ANY)] * len(pieces),
            out_specs=pl.BlockSpec((TABLE_ROWS, DIM), lambda i, *_: (i, 0)),
            scratch_shapes=[
                pltpu.VMEM((NDEV * BLOCK, DIM), F32),
                pltpu.SemaphoreType.DMA((NDEV,)),
            ],
        ),
        compiler_params=pltpu.CompilerParams(vmem_limit_bytes=56 * 1024 * 1024),
        cost_estimate=pl.CostEstimate(flops=80_000_000_000, bytes_accessed=240_000_000, transcendentals=0),
        name='table_build',
    )(starts, entry, place, *pieces)


def dot(a, b, dims):
    return lax.dot_general(a, b, (dims, ((), ())), preferred_element_type=F32)


def solution(mesh):
    def per_device(tok_ids, grad_out, n_real, embed_table, w_in, w_out):
        dev = lax.axis_index('data')
        c, x, y, z = dev % 2, (dev // 2) % 2, (dev // 4) % 2, dev // 8

        pos = jnp.arange(TOK, dtype=jnp.int32)
        seen = (tok_ids[:, None] == tok_ids[None, :]) & (pos[None, :] < pos[:, None])
        first = ~jnp.any(seen, axis=1)
        rank = jnp.sum((tok_ids[None, :] < tok_ids[:, None]) & first[None, :], axis=1, dtype=jnp.int32)
        slot = jnp.arange(UNIQ, dtype=jnp.int32)
        hit = rank[None, :] == slot[:, None]
        uniq = jnp.sum(jnp.where(hit & first[None, :], tok_ids[None, :], 0), axis=1, dtype=jnp.int32)
        pick = (rank[:, None] == slot[None, :]).astype(BF16)
        pick_t = hit.astype(BF16)

        x_uniq = jnp.take(embed_table, uniq, axis=0)
        z_uniq = dot(x_uniq, w_in, ((1,), (0,))).astype(BF16)
        zu = z_uniq.astype(F32)
        h_uniq = (0.5 * zu * (1.0 + jnp.tanh(GELU_C * (zu + GELU_A * zu * zu * zu)))).astype(BF16)

        dy = jnp.where((pos < n_real[0])[:, None], grad_out, jnp.zeros_like(grad_out))

        def act_half(lane):
            return dot(pick, lax.dynamic_slice_in_dim(h_uniq, lane * (FFN // 2), FFN // 2, axis=1), ((1,), (0,))).astype(BF16)

        out_far = dot(act_half(1 - c), dy, ((0,), (0,)))
        out_away = send(out_far, PAIRS_C)
        out_own = dot(act_half(c), dy, ((0,), (0,))) + out_away

        grad_act = dot(dy, w_out, ((1,), (1,))).astype(BF16)
        z_val = dot(pick, z_uniq, ((1,), (0,))).astype(BF16).astype(F32)
        tanh_val = jnp.tanh(GELU_C * (z_val + GELU_A * z_val * z_val * z_val))
        slope = 0.5 * (1.0 + tanh_val) + 0.5 * z_val * (1.0 - tanh_val * tanh_val) * GELU_C * (1.0 + 3.0 * GELU_A * z_val * z_val)
        grad_pre = (grad_act.astype(F32) * slope).astype(BF16)

        def x_half(lane):
            return dot(pick, lax.dynamic_slice_in_dim(x_uniq, lane * (DIM // 2), DIM // 2, axis=1), ((1,), (0,))).astype(BF16)

        in_far = dot(x_half(1 - c), grad_pre, ((0,), (0,)))
        in_away = send(in_far, PAIRS_C)
        in_own = dot(x_half(c), grad_pre, ((0,), (0,))) + in_away

        grad_x = (dy.astype(F32) + dot(grad_pre, w_in, ((1,), (1,)))).astype(BF16)
        summed = dot(pick_t, grad_x, ((1,), (0,)))
        keys = (uniq * NDEV + dev).astype(F32)
        block = jnp.concatenate([summed, jnp.pad(keys[None, :], ((0, 7), (0, DIM - UNIQ)))], axis=0)

        shard_out = scatter_sum(out_own, x, y, z)
        shard_in = scatter_sum(in_own, x, y, z)

        parts = gather_plane(gather_column(block, z))
        grad_table = build_table(parts + cross(parts))

        grad_w_out = gather_weight(shard_out, x, y, z, c)
        grad_w_in = gather_weight(shard_in, x, y, z, c)
        return grad_table, grad_w_in, grad_w_out

    return jax.shard_map(per_device, mesh=mesh, in_specs=(P('data'), P('data', None), P('data'), P(), P(), P()), out_specs=(P(), P(), P()), check_vma=False)
```

time: 1190 us -> 787 us (0.66)
  other arithmetic: 724 us -> 32 us
  waiting for transfers between devices: 259 us -> 392 us
  Pallas kernels: 0 us -> 92.7 us
  starting transfers between devices: 0.08 us -> 85.2 us
  blocking collectives: 55.3 us -> 0 us
  local copies, waits for them, and re-layouts: 38 us -> 79.8 us
  between operations: 15.1 us -> 2.49 us
    scatter-add x3 -> x0, other arithmetic: 655 us -> none  [per_device(): jax.ops.segment_sum(all_rows.astype(jnp.float32), all_ids, num_segments=e...]
    ppermute x0 -> x67, waiting for transfers between devices: none -> 392 us  [send(): return lax.ppermute(arr, 'data', pairs)]
    all_gather x1 -> x0, waiting for transfers between devices: 259 us -> none  [per_device(): all_rows = lax.all_gather(grad_x, 'data', tiled=True)]
    pallas_call x0 -> x3, Pallas kernels: none -> 92.7 us  [the longest x1 92.7 us: build_table(): pl.pallas_call(table_kernel, out_shape=jax.ShapeDtypeStruct((VOCAB, DIM),...]
    ppermute x0 -> x67, starting transfers between devices: none -> 85.2 us  [send(): return lax.ppermute(arr, 'data', pairs)]
    convert_element_type x1 -> x2, other arithmetic: 67.5 us -> 0.01 us  [the longest x1 0.01 us: per_device(): keys = (uniq * NDEV + dev).astype(F32)]
    all_gather x1 -> x0, blocking collectives: 55.3 us -> none  [per_device(): all_ids = lax.all_gather(tok_ids, 'data', tiled=True)]
    dynamic_update_slice x0 -> x20, local copies, waits for them, and re-layouts: none -> 32.9 us  [gather_weight(): lax.dynamic_update_slice_in_dim(out, p.reshape(-1, width), lane * 32 * k...]
  transfers between devices with their start and end apart: 2 -> 67, of which waited for: 1 -> 25; matrix products, arithmetic and copies ran while one was open for 64% -> 19% of each run, Pallas kernels for 0% -> 12%
where the time goes in v1:
time: 787 us; the launch traced here: 780 us
  waiting for transfers between devices  392 us (50%)
  matrix products  95.9 us (12%)
  Pallas kernels  92.7 us (12%)
  starting transfers between devices  85.2 us (11%)
  local copies, waits for them, and re-layouts  79.8 us (10%)
  other arithmetic  32 us (4%)
    ppermute x67, waiting for transfers between devices, send(): return lax.ppermute(arr, 'data', pairs)  392 us
    dot_general x8, matrix products, dot(): return lax.dot_general(a, b, (dims, ((), ())), preferred_element_type=F32)  95.9 us
    pallas_call x1, Pallas kernels, build_table(): pl.pallas_call(table_kernel, out_shape=jax.ShapeDtypeStruct((VOCAB, DIM),...  92.7 us
    ppermute x67, starting transfers between devices, send(): return lax.ppermute(arr, 'data', pairs)  85.2 us
    dynamic_update_slice x20, local copies, waits for them, and re-layouts, gather_weight(): lax.dynamic_update_slice_in_dim(out, p.reshape(-1, width), lane * 32 * k...  32.9 us
  transfers between devices with their start and end apart: 67, of which 25 were waited for; matrix products, arithmetic and copies ran while one was open for 19% of the time, Pallas kernels for 12%

profile of v1, /device:TPU:0, one launch (start us, length us, event | category | flops | bytes accessed | tf_op | source)
XLA Modules:
  0.0 779.7 jit_solution(14203923206880343669)
XLA Ops:
  5.1 3.2 gather_fusion
  8.5 8.9 %fusion.10 = (bf16[256,4096]{1,0:T(8,128)(2,1)}, bf16[256,4096]{1,0:T(8,128)(2,1)}) fusion(bf16[256,1024]{1,0:T(8,128)(2,1)S(1)} %broadcast_select_fusion.1, bf16[1024,4096]{1,0:T(8,128)(2,1)} %param.10), kind=kOutput, calls=%fused_computation.53 | convolution fusion | flops 2159017984 | bytes 13107200 | tf_op jit(solution)/shard_map/dot_general | solution.py:193
  17.4 11.5 %fusion.111 = bf16[1024,4096]{1,0:T(8,128)(2,1)} fusion(bf16[4096,1024]{1,0:T(8,128)(2,1)S(1)} %bitcast.180, bf16[1024,1024]{1,0:T(8,128)(2,1)S(1)} %copy-done.10, pred[1024]{0:T(1024)(128)(4,1)S(1)} %iota_compare_fusion.14), kind=kOutput, calls=%fused_computation.237 | convolution fusion | flops 8590983168 | bytes 18875392 | tf_op jit(solution)/shard_map/dot_general | solution.py:193
  28.9 16.3 %fusion.7 = bf16[1024,4096]{1,0:T(8,128)(2,1)} fusion(bf16[1024,4096]{1,0:T(8,128)(2,1)} %fusion.111, bf16[256,4096]{1,0:T(8,128)(2,1)} %get-tuple-element.26, s32[1024]{0:T(1024)S(1)} %convert_reduce_fusion), kind=kOutput, calls=%fused_computation.15 | convolution fusion | flops 2240020480 | bytes 18878464 | tf_op jit(solution)/shard_map/dot_general | solution.py:193
  45.2 9.8 %fusion.30 = f32[512,4096]{1,0:T(8,128)} fusion(bf16[1024,4096]{1,0:T(8,128)(2,1)} %fusion.7, s32[1024]{0:T(1024)S(1)} %convert_reduce_fusion, bf16[256,1024]{1,0:T(8,128)(2,1)S(1)} %broadcast_select_fusion.1, s32[]{:T(128)S(6)} %select_n.218), kind=kOutput, calls=%fused_computation.75 | convolution fusion | flops 4564189184 | bytes 17043460 | tf_op jit(solution)/shard_map/dot_general | solution.py:193
  55.6 10.3 %fusion.14 = f32[2048,1024]{1,0:T(8,128)} fusion(bf16[256,4096]{1,0:T(8,128)(2,1)} %get-tuple-element.25, s32[]{:T(128)S(6)} %select_n.238, s32[1024]{0:T(1024)S(1)} %convert_reduce_fusion, bf16[1024,1024]{1,0:T(8,128)(2,1)S(1)} %copy-done.10, pred[1024]{0:T(1024)(128)(4,1)S(1)} %iota_compare_fusion.14), kind=kOutput, calls=%fused_computation.57 | convolution fusion | flops 5372116992 | bytes 11539460 | tf_op jit(solution)/shard_map/dot_general | solution.py:193
  65.9 14.4 %fusion.27 = f32[256,1024]{1,0:T(8,128)S(1)} fusion(bf16[1024,4096]{1,0:T(8,128)(2,1)} %fusion.7, bf16[1024,4096]{1,0:T(8,128)(2,1)} %param.10, s32[1024]{0:T(1024)S(1)} %convert_reduce_fusion, bf16[1024,1024]{1,0:T(8,128)(2,1)S(1)} %copy-done.10, pred[1024]{0:T(1024)(128)(4,1)S(1)} %iota_compare_fusion.14), kind=kOutput, calls=%fused_computation.69 | convolution fusion | flops 9131261952 | bytes 19928064 | tf_op jit(solution)/shard_map/dot_general | solution.py:193
  80.4 5.0 collective-permute-start
  86.8 21.9 %collective-permute-done = f32[264,1024]{1,0:T(8,128)S(1)} collective-permute-done((f32[264,1024]{1,0:T(8,128)S(1)}, f32[264,1024]{1,0:T(8,128)S(1)}, u32[]{:S(2)}, u32[]{:S(2)}) %collective-permute-start) | collective-permute-done | bytes 1081376 | tf_op jit(solution)/shard_map/ppermute | solution.py:46
  115.9 24.8 %collective-permute-done.4 = f32[264,1024]{1,0:T(8,128)} collective-permute-done((f32[264,1024]{1,0:T(8,128)S(1)}, f32[264,1024]{1,0:T(8,128)}, u32[]{:S(2)}, u32[]{:S(2)}) %collective-permute-start.4) | collective-permute-done | bytes 1081376 | tf_op jit(solution)/shard_map/ppermute | solution.py:46
  146.2 20.6 %collective-permute-done.5 = f32[264,1024]{1,0:T(8,128)S(1)} collective-permute-done((f32[264,1024]{1,0:T(8,128)}, f32[264,1024]{1,0:T(8,128)S(1)}, u32[]{:S(2)}, u32[]{:S(2)}) %collective-permute-start.5) | collective-permute-done | bytes 1081376 | tf_op jit(solution)/shard_map/ppermute | solution.py:46
  174.2 11.3 %convolution_add_fusion = f32[512,4096]{1,0:T(8,128)} fusion(f32[512,4096]{1,0:T(8,128)} %collective-permute-done.15, bf16[1024,4096]{1,0:T(8,128)(2,1)} %fusion.7, s32[1024]{0:T(1024)S(1)} %convert_reduce_fusion, bf16[256,1024]{1,0:T(8,128)(2,1)S(1)} %copy-done.7, s32[]{:T(128)S(6)} %select_n.217), kind=kOutput, calls=%fused_computation.22 | convolution fusion | flops 4566286336 | bytes 25432068 | tf_op jit(solution)/shard_map/dot_general | solution.py:193
  185.4 3.2 constant_dynamic-slice_fusion.5
  189.2 3.1 constant_dynamic-slice_fusion.6
  192.8 13.4 %fusion.20 = f32[2048,1024]{1,0:T(8,128)} fusion(f32[2048,1024]{1,0:T(8,128)} %collective-permute-done.41, bf16[256,4096]{1,0:T(8,128)(2,1)} %get-tuple-element.25, s32[]{:T(128)S(6)} %select_n.237, s32[1024]{0:T(1024)S(1)} %convert_reduce_fusion, bf16[1024,1024]{1,0:T(8,128)(2,1)} %param.7, pred[1024]{0:T(1024)(128)(4,1)S(1)} %iota_compare_fusion.14), kind=kOutput, calls=%fused_computation.66 | convolution fusion | flops 5374214144 | bytes 19928068 | tf_op jit(solution)/shard_map/dot_general | solution.py:193
  206.2 3.2 constant_dynamic-slice_fusion.2
  210.9 103.2 %collective-permute-done.18 = f32[2,1,4,1,16,4096]{5,4,3,2,1,0:T(8,128)} collective-permute-done((f32[2,1,4,1,16,4096]{5,4,3,2,1,0:T(8,128)}, f32[2,1,4,1,16,4096]{5,4,3,2,1,0:T(8,128)}, u32[]{:S(2)}, u32[]{:S(2)}) %collective-permute-start.18) | collective-permute-done | bytes 2097184 | tf_op jit(solution)/shard_map/ppermute | solution.py:46
  316.4 3.9 constant_dynamic-slice_fusion.3
  320.3 35.0 %collective-permute-done.44 = f32[2,1,4,1,64,1024]{5,4,3,2,1,0:T(8,128)} collective-permute-done((f32[2,1,4,1,64,1024]{5,4,3,2,1,0:T(8,128)}, f32[2,1,4,1,64,1024]{5,4,3,2,1,0:T(8,128)}, u32[]{:S(2)}, u32[]{:S(2)}) %collective-permute-start.44) | collective-permute-done | bytes 2097184 | tf_op jit(solution)/shard_map/ppermute | solution.py:46
  360.1 3.4 add_add_fusion.2
  365.0 3.2 slice.76
  368.8 3.2 slice.78
  372.0 32.1 %collective-permute-done.42 = f32[1,2,4,1,64,1024]{5,4,3,2,1,0:T(8,128)} collective-permute-done((f32[1,2,4,1,64,1024]{5,4,3,2,1,0:T(8,128)}, f32[1,2,4,1,64,1024]{5,4,3,2,1,0:T(8,128)}, u32[]{:S(2)}, u32[]{:S(2)}) %collective-permute-start.42) | collective-permute-done | bytes 2097184 | tf_op jit(solution)/shard_map/ppermute | solution.py:46
  405.7 21.0 %collective-permute-done.45 = f32[1,1,4,1,64,1024]{5,4,3,2,1,0:T(8,128)} collective-permute-done((f32[1,1,4,1,64,1024]{5,4,3,2,1,0:T(8,128)}, f32[1,1,4,1,64,1024]{5,4,3,2,1,0:T(8,128)}, u32[]{:S(2)}, u32[]{:S(2)}) %collective-permute-start.45) | collective-permute-done | bytes 1048608 | tf_op jit(solution)/shard_map/ppermute | solution.py:46
  434.5 33.9 %collective-permute-done.8.refs_3_ = f32[2,264,1024]{2,1,0:T(8,128)} collective-permute-done((f32[2,264,1024]{2,1,0:T(8,128)}, f32[2,264,1024]{2,1,0:T(8,128)}, u32[]{:S(2)}, u32[]{:S(2)}) %collective-permute-start.8) | collective-permute-done | bytes 2162720 | tf_op jit(solution)/shard_map/ppermute | solution.py:46
  476.2 8.4 %collective-permute-done.46 = f32[2,64,1024]{2,1,0:T(8,128)} collective-permute-done((f32[2,64,1024]{2,1,0:T(8,128)S(1)}, f32[2,64,1024]{2,1,0:T(8,128)}, u32[]{:S(2)}, u32[]{:S(2)}) %collective-permute-start.46) | collective-permute-done | bytes 524320 | tf_op jit(solution)/shard_map/ppermute | solution.py:46
  484.7 5.3 collective-permute-start.21
  494.5 6.0 collective-permute-done.21
  500.5 4.4 collective-permute-start.47
  507.0 8.0 %collective-permute-done.47 = f32[2,64,1024]{2,1,0:T(8,128)S(1)} collective-permute-done((f32[2,64,1024]{2,1,0:T(8,128)S(1)}, f32[2,64,1024]{2,1,0:T(8,128)S(1)}, u32[]{:S(2)}, u32[]{:S(2)}) %collective-permute-start.47) | collective-permute-done | bytes 524320 | tf_op jit(solution)/shard_map/ppermute | solution.py:46
  516.3 5.3 collective-permute-start.22
  524.8 4.6 collective-permute-done.25
  530.8 4.4 collective-permute-start.48
  536.1 3.6 collective-permute-start.26
  543.7 3.8 collective-permute-done.48
  547.6 4.4 collective-permute-start.52
  553.4 5.5 collective-permute-done.26
  560.9 6.9 sort.23
  573.6 14.5 %collective-permute-done.30 = f32[2,16,4096]{2,1,0:T(8,128)S(1)} collective-permute-done((f32[2,16,4096]{2,1,0:T(8,128)}, f32[2,16,4096]{2,1,0:T(8,128)S(1)}, u32[]{:S(2)}, u32[]{:S(2)}) %collective-permute-start.30) | collective-permute-done | bytes 524320 | tf_op jit(solution)/shard_map/ppermute | solution.py:46
  590.1 9.2 %collective-permute-done.56 = f32[2,64,1024]{2,1,0:T(8,128)S(1)} collective-permute-done((f32[2,64,1024]{2,1,0:T(8,128)S(1)}, f32[2,64,1024]{2,1,0:T(8,128)S(1)}, u32[]{:S(2)}, u32[]{:S(2)}) %collective-permute-start.56) | collective-permute-done | bytes 524320 | tf_op jit(solution)/shard_map/ppermute | solution.py:46
  603.2 3.9 collective-permute-done.31
  615.0 92.7 %table_build.1 = f32[50265,1024]{1,0:T(8,128)} custom-call(s32[51]{0:T(128)} %convert_reduce_fusion.1.start_ref, s32[8192]{0:T(1024)} %fusion.100.entry_ref, s32[8192]{0:T(1024)} %get-tuple-element.8.row_ref, f32[4,264,1024]{2,1,0:T(8,128)} %constant_dynamic-slice_fusion.7.refs_0_, f32[4,264,1024]{2,1,0:T(8,128)} %collective-permute-done.6.refs_1_, ...), custom_call_target="tpu_custom_call" | custom-call | flops 80000000000 | bytes 240000000 | tf_op jit(solution)/shard_map/table_build/pallas_call | solution.py:173
  716.3 3.1 constant_dynamic-update-slice_fusion.15
  723.8 11.7 %collective-permute-done.34 = f32[2,2,16,4096]{3,2,1,0:T(8,128)S(1)} collective-permute-done((f32[2,2,16,4096]{3,2,1,0:T(8,128)S(1)}, f32[2,2,16,4096]{3,2,1,0:T(8,128)S(1)}, u32[]{:S(2)}, u32[]{:S(2)}) %collective-permute-start.34) | collective-permute-done | bytes 1048608 | tf_op jit(solution)/shard_map/ppermute | solution.py:46
  735.5 3.2 constant_dynamic-update-slice_fusion.5
  739.9 3.2 constant_dynamic-update-slice_fusion.4
  743.1 14.4 %collective-permute-done.60 = f32[2,2,64,1024]{3,2,1,0:T(8,128)S(1)} collective-permute-done((f32[2,2,64,1024]{3,2,1,0:T(8,128)S(1)}, f32[2,2,64,1024]{3,2,1,0:T(8,128)S(1)}, u32[]{:S(2)}, u32[]{:S(2)}) %collective-permute-start.60) | collective-permute-done | bytes 1048608 | tf_op jit(solution)/shard_map/ppermute | solution.py:46
  762.7 3.2 constant_dynamic-update-slice_fusion.1
  (233 shorter events, 127.8 us)
Async XLA Ops:
  55.0 119.2 %collective-permute-start.15 = (f32[512,4096]{1,0:T(8,128)}, f32[512,4096]{1,0:T(8,128)}, u32[]{:S(2)}, u32[]{:S(2)}) collective-permute-start(f32[512,4096]{1,0:T(8,128)} %fusion.30), channel_id=1, source_target_pairs={{0,1},{1,0},{2,3},{3,2},{4,5},{5,4},{6,7},{7,6},{8,9},{9,8},{10,11... | collective-permute-start | bytes 25165832 | tf_op jit(solution)/shard_map/ppermute | solution.py:46
  65.9 126.9 %collective-permute-start.41 = (f32[2048,1024]{1,0:T(8,128)}, f32[2048,1024]{1,0:T(8,128)}, u32[]{:S(2)}, u32[]{:S(2)}) collective-permute-start(f32[2048,1024]{1,0:T(8,128)} %fusion.14), channel_id=1, source_target_pairs={{0,1},{1,0},{2,3},{3,2},{4,5},{5,4},{6,7},{7,6},{8,9},{9,8},{10,11... | collective-permute-start | bytes 25165832 | tf_op jit(solution)/shard_map/ppermute | solution.py:46
  80.4 28.3 %collective-permute-start = (f32[264,1024]{1,0:T(8,128)S(1)}, f32[264,1024]{1,0:T(8,128)S(1)}, u32[]{:S(2)}, u32[]{:S(2)}) collective-permute-start(f32[264,1024]{1,0:T(8,128)S(1)} %select_maximum_fusion), channel_id=1, source_target_pairs={{0,8},{1,9},{2,10},{3,11},{4,12},{5,13},{6,14},{7,15},{8,16},{9,17... | collective-permute-start | bytes 3244040 | tf_op jit(solution)/shard_map/ppermute | solution.py:46
  85.5 27.4 %collective-permute-start.3 = (f32[264,1024]{1,0:T(8,128)S(1)}, f32[264,1024]{1,0:T(8,128)S(1)}, u32[]{:S(2)}, u32[]{:S(2)}) collective-permute-start(f32[264,1024]{1,0:T(8,128)S(1)} %select_maximum_fusion), channel_id=1, source_target_pairs={{8,0},{9,1},{10,2},{11,3},{12,4},{13,5},{14,6},{15,7},{16,8},{17,9... | collective-permute-start | bytes 3244040 | tf_op jit(solution)/shard_map/ppermute | solution.py:46
  112.9 27.7 %collective-permute-start.4 = (f32[264,1024]{1,0:T(8,128)S(1)}, f32[264,1024]{1,0:T(8,128)}, u32[]{:S(2)}, u32[]{:S(2)}) collective-permute-start(f32[264,1024]{1,0:T(8,128)S(1)} %collective-permute-done.3), channel_id=1, source_target_pairs={{8,0},{9,1},{10,2},{11,3},{12,4},{13,5},{14,6},{15,7},{16,8},{17,9... | collective-permute-start | bytes 3244040 | tf_op jit(solution)/shard_map/ppermute | solution.py:46
  114.2 27.7 %collective-permute-start.2 = (f32[264,1024]{1,0:T(8,128)}, f32[264,1024]{1,0:T(8,128)}, u32[]{:S(2)}, u32[]{:S(2)}) collective-permute-start(f32[264,1024]{1,0:T(8,128)} %collective-permute-done.1), channel_id=1, source_target_pairs={{16,24},{17,25},{18,26},{19,27},{20,28},{21,29},{22,30},{23,31}} | collective-permute-start | bytes 3244040 | tf_op jit(solution)/shard_map/ppermute | solution.py:46
  140.6 26.2 %collective-permute-start.5 = (f32[264,1024]{1,0:T(8,128)}, f32[264,1024]{1,0:T(8,128)S(1)}, u32[]{:S(2)}, u32[]{:S(2)}) collective-permute-start(f32[264,1024]{1,0:T(8,128)} %collective-permute-done.4), channel_id=1, source_target_pairs={{8,0},{9,1},{10,2},{11,3},{12,4},{13,5},{14,6},{15,7}} | collective-permute-start | bytes 3244040 | tf_op jit(solution)/shard_map/ppermute | solution.py:46
  171.2 197.1 %collective-permute-start.6 = (f32[4,264,1024]{2,1,0:T(8,128)}, f32[4,264,1024]{2,1,0:T(8,128)}, u32[]{:S(2)}, u32[]{:S(2)}) collective-permute-start(f32[4,264,1024]{2,1,0:T(8,128)} %constant_dynamic-slice_fusion.7.refs_0_), channel_id=1, source_target_pairs={{0,2},{1,3},{2,0},{3,1},{4,6},{5,7},{6,4},{7,5},{8,10},{9,11},{10,... | collective-permute-start | bytes 12976136 | tf_op jit(solution)/shard_map/ppermute | solution.py:46
  172.7 190.8 %collective-permute-start.7 = (f32[4,264,1024]{2,1,0:T(8,128)}, f32[4,264,1024]{2,1,0:T(8,128)}, u32[]{:S(2)}, u32[]{:S(2)}) collective-permute-start(f32[4,264,1024]{2,1,0:T(8,128)} %constant_dynamic-slice_fusion.7.refs_0_), channel_id=1, source_target_pairs={{0,4},{1,5},{2,6},{3,7},{4,0},{5,1},{6,2},{7,3},{8,12},{9,13},{10,... | collective-permute-start | bytes 12976136 | tf_op jit(solution)/shard_map/ppermute | solution.py:46
  188.7 125.5 %collective-permute-start.18 = (f32[2,1,4,1,16,4096]{5,4,3,2,1,0:T(8,128)}, f32[2,1,4,1,16,4096]{5,4,3,2,1,0:T(8,128)}, u32[]{:S(2)}, u32[]{:S(2)}) collective-permute-start(f32[2,1,4,1,16,4096]{5,4,3,2,1,0:T(8,128)} %constant_dynamic-slice_fusion.5), channel_id=1, source_target_pairs={{0,4},{1,5},{2,6},{3,7},{4,0},{5,1},{6,2},{7,3},{8,12},{9,13},{10,... | collective-permute-start | bytes 6291464 | tf_op jit(solution)/shard_map/ppermute | solution.py:46
  192.3 124.1 %collective-permute-start.16 = (f32[1,2,4,1,16,4096]{5,4,3,2,1,0:T(8,128)}, f32[1,2,4,1,16,4096]{5,4,3,2,1,0:T(8,128)S(1)}, u32[]{:S(2)}, u32[]{:S(2)}) collective-permute-start(f32[1,2,4,1,16,4096]{5,4,3,2,1,0:T(8,128)} %constant_dynamic-slice_fusion.6), channel_id=1, source_target_pairs={{0,2},{1,3},{2,0},{3,1},{4,6},{5,7},{6,4},{7,5},{8,10},{9,11},{10,... | collective-permute-start | bytes 6291464 | tf_op jit(solution)/shard_map/ppermute | solution.py:46
  209.4 145.9 %collective-permute-start.44 = (f32[2,1,4,1,64,1024]{5,4,3,2,1,0:T(8,128)}, f32[2,1,4,1,64,1024]{5,4,3,2,1,0:T(8,128)}, u32[]{:S(2)}, u32[]{:S(2)}) collective-permute-start(f32[2,1,4,1,64,1024]{5,4,3,2,1,0:T(8,128)} %constant_dynamic-slice_fusion.2), channel_id=1, source_target_pairs={{0,4},{1,5},{2,6},{3,7},{4,0},{5,1},{6,2},{7,3},{8,12},{9,13},{10,... | collective-permute-start | bytes 6291464 | tf_op jit(solution)/shard_map/ppermute | solution.py:46
  315.8 42.8 %collective-permute-start.19 = (f32[1,1,4,1,16,4096]{5,4,3,2,1,0:T(8,128)S(1)}, f32[1,1,4,1,16,4096]{5,4,3,2,1,0:T(8,128)}, u32[]{:S(2)}, u32[]{:S(2)}) collective-permute-start(f32[1,1,4,1,16,4096]{5,4,3,2,1,0:T(8,128)S(1)} %dynamic-slice_add_fusion.2), channel_id=1, source_target_pairs={{0,2},{1,3},{2,0},{3,1},{4,6},{5,7},{6,4},{7,5},{8,10},{9,11},{10,... | collective-permute-start | bytes 3145736 | tf_op jit(solution)/shard_map/ppermute | solution.py:46
  316.4 116.4 %collective-permute-start.10 = (f32[4,264,1024]{2,1,0:T(8,128)}, f32[4,264,1024]{2,1,0:T(8,128)}, u32[]{:S(2)}, u32[]{:S(2)}) collective-permute-start(f32[4,264,1024]{2,1,0:T(8,128)} %constant_dynamic-slice_fusion.7.refs_0_), channel_id=1, source_target_pairs={{0,1},{1,0},{2,3},{3,2},{4,5},{5,4},{6,7},{7,6},{8,9},{9,8},{10,11... | collective-permute-start | bytes 12976136 | tf_op jit(solution)/shard_map/ppermute | solution.py:46
  355.3 48.8 %collective-permute-start.42 = (f32[1,2,4,1,64,1024]{5,4,3,2,1,0:T(8,128)}, f32[1,2,4,1,64,1024]{5,4,3,2,1,0:T(8,128)}, u32[]{:S(2)}, u32[]{:S(2)}) collective-permute-start(f32[1,2,4,1,64,1024]{5,4,3,2,1,0:T(8,128)} %constant_dynamic-slice_fusion.3), channel_id=1, source_target_pairs={{0,2},{1,3},{2,0},{3,1},{4,6},{5,7},{6,4},{7,5},{8,10},{9,11},{10,... | collective-permute-start | bytes 6291464 | tf_op jit(solution)/shard_map/ppermute | solution.py:46
  358.6 68.0 %collective-permute-start.45 = (f32[1,1,4,1,64,1024]{5,4,3,2,1,0:T(8,128)}, f32[1,1,4,1,64,1024]{5,4,3,2,1,0:T(8,128)}, u32[]{:S(2)}, u32[]{:S(2)}) collective-permute-start(f32[1,1,4,1,64,1024]{5,4,3,2,1,0:T(8,128)} %dynamic-slice_add_fusion), channel_id=1, source_target_pairs={{0,2},{1,3},{2,0},{3,1},{4,6},{5,7},{6,4},{7,5},{8,10},{9,11},{10,... | collective-permute-start | bytes 3145736 | tf_op jit(solution)/shard_map/ppermute | solution.py:46
  363.5 66.2 %collective-permute-start.17 = (f32[1,1,4,1,16,4096]{5,4,3,2,1,0:T(8,128)}, f32[1,1,4,1,16,4096]{5,4,3,2,1,0:T(8,128)S(1)}, u32[]{:S(2)}, u32[]{:S(2)}) collective-permute-start(f32[1,1,4,1,16,4096]{5,4,3,2,1,0:T(8,128)} %get-tuple-element.12), channel_id=1, source_target_pairs={{0,4},{1,5},{2,6},{3,7},{4,0},{5,1},{6,2},{7,3},{8,12},{9,13},{10,... | collective-permute-start | bytes 3145736 | tf_op jit(solution)/shard_map/ppermute | solution.py:46
  368.2 100.1 %collective-permute-start.8 = (f32[2,264,1024]{2,1,0:T(8,128)}, f32[2,264,1024]{2,1,0:T(8,128)}, u32[]{:S(2)}, u32[]{:S(2)}) collective-permute-start(f32[2,264,1024]{2,1,0:T(8,128)} %slice.76), channel_id=1, source_target_pairs={{0,2},{1,3},{2,0},{3,1},{4,6},{5,7},{6,4},{7,5},{8,10},{9,11},{10,... | collective-permute-start | bytes 6488072 | tf_op jit(solution)/shard_map/ppermute | solution.py:46
  404.1 90.3 %collective-permute-start.9 = (f32[2,264,1024]{2,1,0:T(8,128)}, f32[2,264,1024]{2,1,0:T(8,128)}, u32[]{:S(2)}, u32[]{:S(2)}) collective-permute-start(f32[2,264,1024]{2,1,0:T(8,128)} %slice.78), channel_id=1, source_target_pairs={{0,4},{1,5},{2,6},{3,7},{4,0},{5,1},{6,2},{7,3},{8,12},{9,13},{10,... | collective-permute-start | bytes 6488072 | tf_op jit(solution)/shard_map/ppermute | solution.py:46
  426.6 80.3 %collective-permute-start.11 = (f32[4,264,1024]{2,1,0:T(8,128)}, f32[4,264,1024]{2,1,0:T(8,128)}, u32[]{:S(2)}, u32[]{:S(2)}) collective-permute-start(f32[4,264,1024]{2,1,0:T(8,128)} %collective-permute-done.6.refs_1_), channel_id=1, source_target_pairs={{0,1},{1,0},{2,3},{3,2},{4,5},{5,4},{6,7},{7,6},{8,9},{9,8},{10,11... | collective-permute-start | bytes 12976136 | tf_op jit(solution)/shard_map/ppermute | solution.py:46
  429.7 39.5 %collective-permute-start.43 = (f32[1,1,4,1,64,1024]{5,4,3,2,1,0:T(8,128)S(1)}, f32[1,1,4,1,64,1024]{5,4,3,2,1,0:T(8,128)S(1)}, u32[]{:S(2)}, u32[]{:S(2)}) collective-permute-start(f32[1,1,4,1,64,1024]{5,4,3,2,1,0:T(8,128)S(1)} %get-tuple-element.10), channel_id=1, source_target_pairs={{0,4},{1,5},{2,6},{3,7},{4,0},{5,1},{6,2},{7,3},{8,12},{9,13},{10,... | collective-permute-start | bytes 3145736 | tf_op jit(solution)/shard_map/ppermute | solution.py:46
  432.9 38.4 %collective-permute-start.20 = (f32[2,16,4096]{2,1,0:T(8,128)S(1)}, f32[2,16,4096]{2,1,0:T(8,128)S(1)}, u32[]{:S(2)}, u32[]{:S(2)}) collective-permute-start(f32[2,16,4096]{2,1,0:T(8,128)S(1)} %get-tuple-element.23), channel_id=1, source_target_pairs={{0,8},{1,9},{2,10},{3,11},{4,12},{5,13},{6,14},{7,15}} | collective-permute-start | bytes 1572872 | tf_op jit(solution)/shard_map/ppermute | solution.py:46
  469.2 66.9 %collective-permute-start.12 = (f32[4,264,1024]{2,1,0:T(8,128)}, f32[4,264,1024]{2,1,0:T(8,128)}, u32[]{:S(2)}, u32[]{:S(2)}) collective-permute-start(f32[4,264,1024]{2,1,0:T(8,128)} %collective-permute-done.7.refs_2_), channel_id=1, source_target_pairs={{0,1},{1,0},{2,3},{3,2},{4,5},{5,4},{6,7},{7,6},{8,9},{9,8},{10,11... | collective-permute-start | bytes 12976136 | tf_op jit(solution)/shard_map/ppermute | solution.py:46
  494.4 57.6 %collective-permute-start.13 = (f32[2,264,1024]{2,1,0:T(8,128)}, f32[2,264,1024]{2,1,0:T(8,128)S(1)}, u32[]{:S(2)}, u32[]{:S(2)}) collective-permute-start(f32[2,264,1024]{2,1,0:T(8,128)} %collective-permute-done.8.refs_3_), channel_id=1, source_target_pairs={{0,1},{1,0},{2,3},{3,2},{4,5},{5,4},{6,7},{7,6},{8,9},{9,8},{10,11... | collective-permute-start | bytes 6488072 | tf_op jit(solution)/shard_map/ppermute | solution.py:46
  506.9 52.6 %collective-permute-start.14 = (f32[2,264,1024]{2,1,0:T(8,128)}, f32[2,264,1024]{2,1,0:T(8,128)S(1)}, u32[]{:S(2)}, u32[]{:S(2)}) collective-permute-start(f32[2,264,1024]{2,1,0:T(8,128)} %collective-permute-done.9.refs_4_), channel_id=1, source_target_pairs={{0,1},{1,0},{2,3},{3,2},{4,5},{5,4},{6,7},{7,6},{8,9},{9,8},{10,11... | collective-permute-start | bytes 6488072 | tf_op jit(solution)/shard_map/ppermute | solution.py:46
  530.8 16.7 %collective-permute-start.48 = (f32[2,64,1024]{2,1,0:T(8,128)S(1)}, f32[2,64,1024]{2,1,0:T(8,128)S(1)}, u32[]{:S(2)}, u32[]{:S(2)}) collective-permute-start(f32[2,64,1024]{2,1,0:T(8,128)S(1)} %get-tuple-element.13), channel_id=1, source_target_pairs={{0,8},{1,9},{2,10},{3,11},{4,12},{5,13},{6,14},{7,15},{8,16},{9,17... | collective-permute-start | bytes 1572872 | tf_op jit(solution)/shard_map/ppermute | solution.py:46
  536.1 22.7 %collective-permute-start.26 = (f32[2,16,4096]{2,1,0:T(8,128)}, f32[2,16,4096]{2,1,0:T(8,128)S(1)}, u32[]{:S(2)}, u32[]{:S(2)}) collective-permute-start(f32[2,16,4096]{2,1,0:T(8,128)} %fusion.61), channel_id=1, source_target_pairs={{0,8},{1,9},{2,10},{3,11},{4,12},{5,13},{6,14},{7,15},{8,16},{9,17... | collective-permute-start | bytes 1572872 | tf_op jit(solution)/shard_map/ppermute | solution.py:46
  542.4 25.4 %collective-permute-start.29 = (f32[2,16,4096]{2,1,0:T(8,128)}, f32[2,16,4096]{2,1,0:T(8,128)}, u32[]{:S(2)}, u32[]{:S(2)}) collective-permute-start(f32[2,16,4096]{2,1,0:T(8,128)} %fusion.61), channel_id=1, source_target_pairs={{8,0},{9,1},{10,2},{11,3},{12,4},{13,5},{14,6},{15,7},{16,8},{17,9... | collective-permute-start | bytes 1572872 | tf_op jit(solution)/shard_map/ppermute | solution.py:46
  547.6 21.5 %collective-permute-start.52 = (f32[2,64,1024]{2,1,0:T(8,128)S(1)}, f32[2,64,1024]{2,1,0:T(8,128)S(1)}, u32[]{:S(2)}, u32[]{:S(2)}) collective-permute-start(f32[2,64,1024]{2,1,0:T(8,128)S(1)} %fusion.41), channel_id=1, source_target_pairs={{0,8},{1,9},{2,10},{3,11},{4,12},{5,13},{6,14},{7,15},{8,16},{9,17... | collective-permute-start | bytes 1572872 | tf_op jit(solution)/shard_map/ppermute | solution.py:46
  552.1 17.8 %collective-permute-start.55 = (f32[2,64,1024]{2,1,0:T(8,128)S(1)}, f32[2,64,1024]{2,1,0:T(8,128)S(1)}, u32[]{:S(2)}, u32[]{:S(2)}) collective-permute-start(f32[2,64,1024]{2,1,0:T(8,128)S(1)} %fusion.41), channel_id=1, source_target_pairs={{8,0},{9,1},{10,2},{11,3},{12,4},{13,5},{14,6},{15,7},{16,8},{17,9... | collective-permute-start | bytes 1572872 | tf_op jit(solution)/shard_map/ppermute | solution.py:46
  567.8 20.2 %collective-permute-start.30 = (f32[2,16,4096]{2,1,0:T(8,128)}, f32[2,16,4096]{2,1,0:T(8,128)S(1)}, u32[]{:S(2)}, u32[]{:S(2)}) collective-permute-start(f32[2,16,4096]{2,1,0:T(8,128)} %collective-permute-done.29), channel_id=1, source_target_pairs={{8,0},{9,1},{10,2},{11,3},{12,4},{13,5},{14,6},{15,7},{16,8},{17,9... | collective-permute-start | bytes 1572872 | tf_op jit(solution)/shard_map/ppermute | solution.py:46
  569.2 20.2 %collective-permute-start.53 = (f32[2,64,1024]{2,1,0:T(8,128)S(1)}, f32[2,64,1024]{2,1,0:T(8,128)S(1)}, u32[]{:S(2)}, u32[]{:S(2)}) collective-permute-start(f32[2,64,1024]{2,1,0:T(8,128)S(1)} %collective-permute-done.52), channel_id=1, source_target_pairs={{8,16},{9,17},{10,18},{11,19},{12,20},{13,21},{14,22},{15,23},{16,... | collective-permute-start | bytes 1572872 | tf_op jit(solution)/shard_map/ppermute | solution.py:46
  569.9 29.5 %collective-permute-start.56 = (f32[2,64,1024]{2,1,0:T(8,128)S(1)}, f32[2,64,1024]{2,1,0:T(8,128)S(1)}, u32[]{:S(2)}, u32[]{:S(2)}) collective-permute-start(f32[2,64,1024]{2,1,0:T(8,128)S(1)} %collective-permute-done.55), channel_id=1, source_target_pairs={{8,0},{9,1},{10,2},{11,3},{12,4},{13,5},{14,6},{15,7},{16,8},{17,9... | collective-permute-start | bytes 1572872 | tf_op jit(solution)/shard_map/ppermute | solution.py:46
  571.2 29.6 %collective-permute-start.28 = (f32[2,16,4096]{2,1,0:T(8,128)S(1)}, f32[2,16,4096]{2,1,0:T(8,128)S(1)}, u32[]{:S(2)}, u32[]{:S(2)}) collective-permute-start(f32[2,16,4096]{2,1,0:T(8,128)S(1)} %collective-permute-done.27), channel_id=1, source_target_pairs={{16,24},{17,25},{18,26},{19,27},{20,28},{21,29},{22,30},{23,31}} | collective-permute-start | bytes 1572872 | tf_op jit(solution)/shard_map/ppermute | solution.py:46
  588.1 19.0 %collective-permute-start.31 = (f32[2,16,4096]{2,1,0:T(8,128)S(1)}, f32[2,16,4096]{2,1,0:T(8,128)S(1)}, u32[]{:S(2)}, u32[]{:S(2)}) collective-permute-start(f32[2,16,4096]{2,1,0:T(8,128)S(1)} %collective-permute-done.30), channel_id=1, source_target_pairs={{8,0},{9,1},{10,2},{11,3},{12,4},{13,5},{14,6},{15,7}} | collective-permute-start | bytes 1572872 | tf_op jit(solution)/shard_map/ppermute | solution.py:46
  589.4 20.0 %collective-permute-start.54 = (f32[2,64,1024]{2,1,0:T(8,128)S(1)}, f32[2,64,1024]{2,1,0:T(8,128)S(1)}, u32[]{:S(2)}, u32[]{:S(2)}) collective-permute-start(f32[2,64,1024]{2,1,0:T(8,128)S(1)} %collective-permute-done.53), channel_id=1, source_target_pairs={{16,24},{17,25},{18,26},{19,27},{20,28},{21,29},{22,30},{23,31}} | collective-permute-start | bytes 1572872 | tf_op jit(solution)/shard_map/ppermute | solution.py:46
  607.3 105.2 %collective-permute-start.32 = (f32[4,2,16,4096]{3,2,1,0:T(8,128)S(1)}, f32[4,2,16,4096]{3,2,1,0:T(8,128)}, u32[]{:S(2)}, u32[]{:S(2)}) collective-permute-start(f32[4,2,16,4096]{3,2,1,0:T(8,128)S(1)} %constant_dynamic-slice_fusion.4), channel_id=1, source_target_pairs={{0,2},{1,3},{2,0},{3,1},{4,6},{5,7},{6,4},{7,5},{8,10},{9,11},{10,... | collective-permute-start | bytes 6291464 | tf_op jit(solution)/shard_map/ppermute | solution.py:46
  607.9 101.4 %collective-permute-start.33 = (f32[4,2,16,4096]{3,2,1,0:T(8,128)S(1)}, f32[4,2,16,4096]{3,2,1,0:T(8,128)S(1)}, u32[]{:S(2)}, u32[]{:S(2)}) collective-permute-start(f32[4,2,16,4096]{3,2,1,0:T(8,128)S(1)} %constant_dynamic-slice_fusion.4), channel_id=1, source_target_pairs={{0,4},{1,5},{2,6},{3,7},{4,0},{5,1},{6,2},{7,3},{8,12},{9,13},{10,... | collective-permute-start | bytes 6291464 | tf_op jit(solution)/shard_map/ppermute | solution.py:46
  612.9 106.5 %collective-permute-start.58 = (f32[4,2,64,1024]{3,2,1,0:T(8,128)S(1)}, f32[4,2,64,1024]{3,2,1,0:T(8,128)}, u32[]{:S(2)}, u32[]{:S(2)}) collective-permute-start(f32[4,2,64,1024]{3,2,1,0:T(8,128)S(1)} %constant_dynamic-slice_fusion), channel_id=1, source_target_pairs={{0,2},{1,3},{2,0},{3,1},{4,6},{5,7},{6,4},{7,5},{8,10},{9,11},{10,... | collective-permute-start | bytes 6291464 | tf_op jit(solution)/shard_map/ppermute | solution.py:46
  613.5 100.9 %collective-permute-start.59 = (f32[4,2,64,1024]{3,2,1,0:T(8,128)S(1)}, f32[4,2,64,1024]{3,2,1,0:T(8,128)}, u32[]{:S(2)}, u32[]{:S(2)}) collective-permute-start(f32[4,2,64,1024]{3,2,1,0:T(8,128)S(1)} %constant_dynamic-slice_fusion), channel_id=1, source_target_pairs={{0,4},{1,5},{2,6},{3,7},{4,0},{5,1},{6,2},{7,3},{8,12},{9,13},{10,... | collective-permute-start | bytes 6291464 | tf_op jit(solution)/shard_map/ppermute | solution.py:46
  615.0 105.7 %collective-permute-start.62 = (f32[4,2,64,1024]{3,2,1,0:T(8,128)S(1)}, f32[4,2,64,1024]{3,2,1,0:T(8,128)}, u32[]{:S(2)}, u32[]{:S(2)}) collective-permute-start(f32[4,2,64,1024]{3,2,1,0:T(8,128)S(1)} %constant_dynamic-slice_fusion), channel_id=1, source_target_pairs={{0,1},{1,0},{2,3},{3,2},{4,5},{5,4},{6,7},{7,6},{8,9},{9,8},{10,11... | collective-permute-start | bytes 6291464 | tf_op jit(solution)/shard_map/ppermute | solution.py:46
  709.4 26.1 %collective-permute-start.34 = (f32[2,2,16,4096]{3,2,1,0:T(8,128)S(1)}, f32[2,2,16,4096]{3,2,1,0:T(8,128)S(1)}, u32[]{:S(2)}, u32[]{:S(2)}) collective-permute-start(f32[2,2,16,4096]{3,2,1,0:T(8,128)S(1)} %slice.87), channel_id=1, source_target_pairs={{0,2},{1,3},{2,0},{3,1},{4,6},{5,7},{6,4},{7,5},{8,10},{9,11},{10,... | collective-permute-start | bytes 3145736 | tf_op jit(solution)/shard_map/ppermute | solution.py:46
  713.8 26.1 %collective-permute-start.35 = (f32[2,2,16,4096]{3,2,1,0:T(8,128)S(1)}, f32[2,2,16,4096]{3,2,1,0:T(8,128)S(1)}, u32[]{:S(2)}, u32[]{:S(2)}) collective-permute-start(f32[2,2,16,4096]{3,2,1,0:T(8,128)S(1)} %slice.88), channel_id=1, source_target_pairs={{0,4},{1,5},{2,6},{3,7},{4,0},{5,1},{6,2},{7,3},{8,12},{9,13},{10,... | collective-permute-start | bytes 3145736 | tf_op jit(solution)/shard_map/ppermute | solution.py:46
  715.7 41.8 %collective-permute-start.60 = (f32[2,2,64,1024]{3,2,1,0:T(8,128)S(1)}, f32[2,2,64,1024]{3,2,1,0:T(8,128)S(1)}, u32[]{:S(2)}, u32[]{:S(2)}) collective-permute-start(f32[2,2,64,1024]{3,2,1,0:T(8,128)S(1)} %slice.89), channel_id=1, source_target_pairs={{0,2},{1,3},{2,0},{3,1},{4,6},{5,7},{6,4},{7,5},{8,10},{9,11},{10,... | collective-permute-start | bytes 3145736 | tf_op jit(solution)/shard_map/ppermute | solution.py:46
  719.4 47.5 %collective-permute-start.36 = (f32[4,2,16,4096]{3,2,1,0:T(8,128)S(1)}, f32[4,2,16,4096]{3,2,1,0:T(8,128)S(1)}, u32[]{:S(2)}, u32[]{:S(2)}) collective-permute-start(f32[4,2,16,4096]{3,2,1,0:T(8,128)S(1)} %constant_dynamic-slice_fusion.4), channel_id=1, source_target_pairs={{0,1},{1,0},{2,3},{3,2},{4,5},{5,4},{6,7},{7,6},{8,9},{9,8},{10,11... | collective-permute-start | bytes 6291464 | tf_op jit(solution)/shard_map/ppermute | solution.py:46
  720.7 40.9 %collective-permute-start.61 = (f32[2,2,64,1024]{3,2,1,0:T(8,128)S(1)}, f32[2,2,64,1024]{3,2,1,0:T(8,128)S(1)}, u32[]{:S(2)}, u32[]{:S(2)}) collective-permute-start(f32[2,2,64,1024]{3,2,1,0:T(8,128)S(1)} %slice.90), channel_id=1, source_target_pairs={{0,4},{1,5},{2,6},{3,7},{4,0},{5,1},{6,2},{7,3},{8,12},{9,13},{10,... | collective-permute-start | bytes 3145736 | tf_op jit(solution)/shard_map/ppermute | solution.py:46
  735.5 33.4 %collective-permute-start.63 = (f32[4,2,64,1024]{3,2,1,0:T(8,128)}, f32[4,2,64,1024]{3,2,1,0:T(8,128)S(1)}, u32[]{:S(2)}, u32[]{:S(2)}) collective-permute-start(f32[4,2,64,1024]{3,2,1,0:T(8,128)} %collective-permute-done.58), channel_id=1, source_target_pairs={{0,1},{1,0},{2,3},{3,2},{4,5},{5,4},{6,7},{7,6},{8,9},{9,8},{10,11... | collective-permute-start | bytes 6291464 | tf_op jit(solution)/shard_map/ppermute | solution.py:46
  739.9 30.4 %collective-permute-start.64 = (f32[4,2,64,1024]{3,2,1,0:T(8,128)}, f32[4,2,64,1024]{3,2,1,0:T(8,128)S(1)}, u32[]{:S(2)}, u32[]{:S(2)}) collective-permute-start(f32[4,2,64,1024]{3,2,1,0:T(8,128)} %collective-permute-done.59), channel_id=1, source_target_pairs={{0,1},{1,0},{2,3},{3,2},{4,5},{5,4},{6,7},{7,6},{8,9},{9,8},{10,11... | collective-permute-start | bytes 6291464 | tf_op jit(solution)/shard_map/ppermute | solution.py:46
  (32 other events, 527.6 us)
